TPU v7x, 32 devices: a whole 2x2x4 slice. The times are simulated.
32 devices in a mesh: owner: 8 (over z, core), sub: 4 (over y, x).
Axes of the slice: x: 2, y: 2, z: 4, core: 2. Of those that a mesh axis runs over, the one named last changes fastest.
Arguments:
- residual: float32 [256, 4608], P('owner', 'sub'), may hold values from -6 to 6
- counts: int32 [8, 16], P('owner', 'sub'), may hold values from 1 to 36
- assembly: int32 [8, 16, 36, 2304], P('owner', 'sub'), may hold values from 0 to 1, as said below
- level_two: float32 [8, 2304, 2304], P('owner', 'sub'), as said below
- block_inverse: float32 [8, 2304, 144], P('owner', 'sub'), as said below
Outputs:
- corrections: float32 [256, 4608], P('owner', 'sub')
- level_residual: float32 [8, 2304, 256], P('owner', 'sub')
Inputs may be any that keep to these rules, and one draw needn't show every extreme that they name: `assembly`: every row of each [36, 2304] block holds exactly one 1; split the 2304 columns into 4 equal ranges and a group's positions into runs of 4: the 144 rows of one run (live or not) put at most 72 of their 1s into one range, and in every run some range gets exactly 72. `level_two`: each group's matrix is symmetric positive definite. `block_inverse`: each diagonal block is symmetric positive definite.
All inputs are finite; a program needn't handle non-finite values.
Results may differ from a plain program's by a relative error of at most 0.0003.
Values sent between devices are 32-bit elements; how exact they have to be, the bound alone decides.
A program may use at most 64 MiB of HBM per device.

v0:
```python
import functools

import jax
import jax.numpy as jnp
from jax import lax
from jax.experimental import pallas as pl
from jax.experimental.pallas import tpu as pltpu
from jax.sharding import PartitionSpec as P

ITERS = 4
LANES = 128
MESH = pl.DeviceIdType.MESH
F32 = jnp.float32
BF16 = jnp.bfloat16


def split(value):
    high = value.astype(BF16)
    return high, (value - high.astype(F32)).astype(BF16)


def split_cat(value):
    return jnp.concatenate(split(value), axis=1)


def fold(value):
    return value[:, :LANES] + value[:, LANES:]


def rows8(value):
    return jnp.sum(value.reshape(value.shape[0] // 8, 8, value.shape[1]), axis=0)


def dot(left, right):
    return jnp.dot(left, right, preferred_element_type=F32)


def total(acc):
    return jnp.sum(acc, axis=0, keepdims=True)


def kernel(
    dims,
    res_ref,
    counts_ref,
    hot_hbm,
    inv_hbm,
    mat_hbm,
    corr_out,
    resid_out,
    mat,
    mat_hi,
    mat_lo,
    pcat,
    pvec,
    xvec,
    rvec,
    zvec,
    wbuf,
    wlast,
    inv_buf,
    inv_hi,
    inv_lo,
    tbuf,
    send_pieces,
    recv_pieces,
    lbuf,
    lcat,
    xcat,
    pick,
    pw_buf,
    corr_pieces,
    corr_back,
    hot_own,
    tcol,
    mat_sem,
    inv_sem,
    hot_sem,
    sub_send,
    sub_recv,
    small_send,
    small_recv,
    own_send,
    own_recv,
):
    no, ns, rows, width, block, local, rhs = dims
    chunks = rhs // LANES
    nblk = width // block
    per = rows // block
    quota = rhs // no
    mo = lax.axis_index("owner")
    me = lax.axis_index("sub")
    relay = ns == 4
    pending = []

    def at(ref, start, size):
        return ref.at[pl.ds(pl.multiple_of(start, 8), size)]

    def remote(src, dst, ssem, rsem, where):
        return pltpu.make_async_remote_copy(
            src_ref=src, dst_ref=dst, send_sem=ssem, recv_sem=rsem, device_id=where,
            device_id_type=MESH,
        )

    mat_copy = pltpu.make_async_copy(mat_hbm.at[0], mat, mat_sem)
    inv_copy = pltpu.make_async_copy(inv_hbm.at[0], at(inv_buf, me * block, block), inv_sem)
    hot_copy = pltpu.make_async_copy(hot_hbm.at[0], hot_own, hot_sem)
    inv_copy.start()
    hot_copy.start()
    mat_copy.start()

    barrier = pltpu.get_barrier_semaphore()
    for step in range(1, ns):
        pl.semaphore_signal(
            barrier, inc=1, device_id={"sub": lax.rem(me + step, ns)}, device_id_type=MESH
        )
    for step in range(1, no):
        pl.semaphore_signal(
            barrier, inc=1, device_id={"owner": lax.rem(mo + step, no)}, device_id_type=MESH
        )

    piece = local
    for part in range(no):
        send_pieces[part * quota : (part + 1) * quota, :] = res_ref[
            :, part * piece : (part + 1) * piece
        ]
    pl.semaphore_wait(barrier, ns - 1 + no - 1)

    class Gather:
        def __init__(self, index, buf, size, src=None):
            self.index, self.buf, self.size, self.src = index, buf, size, src
            self.copies = []

        def own(self, start, size):
            if self.src is not None:
                return self.src.at[pl.ds(start, size)]
            return at(self.buf, me * self.size + start, size)

        def add(self, kind, src, dst, peer):
            copy = remote(
                src, dst, sub_send.at[self.index, kind], sub_recv.at[self.index, kind],
                {"sub": peer},
            )
            copy.start()
            self.copies.append(copy)
            pending.append(copy)

        def start(self):
            size = self.size
            if relay:
                half = size // 2
                xn = me + 1 - 2 * lax.rem(me, 2)
                yn = lax.rem(me + 2, ns)
                self.xn, self.yn, self.half = xn, yn, half
                for kind, (peer, part) in enumerate(((xn, 0), (yn, 1), (xn, 1), (yn, 0))):
                    self.add(
                        kind, self.own(part * half, half),
                        at(self.buf, me * size + part * half, half), peer,
                    )
            else:
                for step in range(1, ns):
                    self.add(
                        step - 1, self.own(0, size), at(self.buf, me * size, size),
                        lax.rem(me + step, ns),
                    )

        def forward(self):
            if relay:
                size, half = self.size, self.half
                self.copies[0].wait_recv()
                first = at(self.buf, self.xn * size, half)
                self.add(4, first, first, self.yn)
                self.copies[1].wait_recv()
                second = at(self.buf, self.yn * size + half, half)
                self.add(5, second, second, self.xn)

        def finish(self):
            for copy in self.copies[2:] if relay else self.copies:
                copy.wait_recv()

    def small_gather(index, buf, size):
        copies = []
        for step in range(1, ns):
            mine = at(buf, me * size, size)
            copy = remote(
                mine, mine, small_send.at[index, step - 1], small_recv.at[index, step - 1],
                {"sub": lax.rem(me + step, ns)},
            )
            copy.start()
            copies.append(copy)
            pending.append(copy)
        return copies

    def exchange(index, src, dst):
        copies = []
        for step in range(1, no):
            peer = lax.rem(mo + step, no)
            copy = remote(
                at(src, peer * quota, quota), at(dst, mo * quota, quota),
                own_send.at[index, step - 1], own_recv.at[index, step - 1], {"owner": peer},
            )
            copy.start()
            copies.append(copy)
            pending.append(copy)
        mine = pl.ds(pl.multiple_of(mo * quota, 8), quota)
        dst[mine, :] = src[mine, :]
        return copies

    routed = exchange(0, send_pieces, recv_pieces)
    inv_copy.wait()
    inv_gather = Gather(0, inv_buf, block)
    inv_gather.start()

    hot_copy.wait()
    prim, slots = hot_own.shape[0], hot_own.shape[1]
    for q in range(slots):
        acc = jnp.zeros((prim, LANES), F32)
        spot = lax.broadcasted_iota(jnp.int32, (prim, LANES), 1)
        for lane in range(0, width, LANES):
            acc += (hot_own[:, q, lane : lane + LANES] * (spot + lane)).astype(F32)
        value = jnp.sum(acc, axis=1, keepdims=True)
        alive = lax.broadcasted_iota(jnp.int32, (prim, 1), 0) < counts_ref[0, q]
        tcol[q * prim : (q + 1) * prim, :] = jnp.broadcast_to(
            jnp.where(alive, value, -1.0), (prim, LANES)
        )
    tbuf[pl.ds(pl.multiple_of(me * 8, 8), 8), :] = tcol[...].T[:8, :]
    targets = small_gather(0, tbuf, 8)

    for copy in routed:
        copy.wait_recv()
    for c in range(chunks):
        lbuf[pl.ds(pl.multiple_of(me * local, 8), local), c * LANES : (c + 1) * LANES] = (
            recv_pieces[c * LANES : (c + 1) * LANES, :].T
        )
    local_gather = Gather(1, lbuf, local)
    local_gather.start()

    mat_copy.wait()
    strip = 48

    @pl.loop(0, rows // strip)
    def _(t):
        here = pl.ds(pl.multiple_of(t * strip, strip), strip)
        high, low = split(mat[here, :])
        mat_hi[here, :] = high
        mat_lo[here, :] = low

    for lane in range(0, width, 2 * LANES):
        spot = lax.broadcasted_iota(jnp.int32, (local, 2 * LANES), 1).astype(F32) + float(lane)
        pick[:, lane : lane + 2 * LANES] = jnp.where(spot == tcol[:, :1], 1.0, 0.0).astype(BF16)

    inv_gather.forward()
    local_gather.forward()
    inv_gather.finish()

    @pl.loop(0, ns)
    def _(s):
        held = pl.ds(pl.multiple_of(s * block, block), block)
        for q in range(per):
            high, low = split(inv_buf[held, q * block : (q + 1) * block])
            inv_hi[s * per + q] = high
            inv_lo[s * per + q] = low

    for copy in targets:
        copy.wait_recv()
    local_gather.finish()

    @pl.loop(0, ns)
    def _(s):
        here = pl.ds(pl.multiple_of(s * local, local), local)
        for c in range(chunks):
            lcat[here, 2 * c * LANES : 2 * (c + 1) * LANES] = split_cat(
                lbuf[here, c * LANES : (c + 1) * LANES]
            )

    @pl.loop(0, nblk)
    def _(b):
        here = pl.ds(pl.multiple_of(b * block, block), block)
        spot = (lax.broadcasted_iota(jnp.int32, (block, local), 0) + b * block).astype(F32)
        acc = jnp.zeros((block, 2 * rhs), F32)
        for s in range(ns):
            hot = jnp.where(spot == tbuf[s * 8 : s * 8 + 1, :], 1.0, 0.0).astype(BF16)
            acc += dot(hot, lcat[s * local : (s + 1) * local, :])
        for c in range(chunks):
            rvec[c, here, :] = fold(acc[:, 2 * c * LANES : 2 * (c + 1) * LANES])

    group = 4 if nblk % 4 == 0 else 1

    def over_blocks(body):
        def step(t, acc):
            for u in range(group):
                b = t * group + u
                acc = acc + body(b, pl.ds(pl.multiple_of(b * block, block), block))
            return acc

        return lax.fori_loop(0, nblk // group, step, jnp.zeros((8, LANES), F32))

    def precond(b, resid):
        rcat = split_cat(resid)
        return fold(dot(inv_hi[b], rcat) + dot(inv_lo[b], rcat))

    tile = 2 * block if rows % (2 * block) == 0 else block

    def matvec(c, store):
        @pl.loop(0, rows // tile)
        def _(t):
            here = pl.ds(pl.multiple_of(t * tile, tile), tile)
            store(
                t * tile,
                fold(dot(mat_hi[here, :], pcat[c]) + dot(mat_lo[here, :], pcat[c])),
            )

    def send_image(step, c, earlier):
        def store(start, value):
            wbuf[step, c, pl.ds(pl.multiple_of(me * rows + start, 8), tile), :] = value

        matvec(c, store)
        if earlier is not None:
            earlier.forward()
        gather = Gather(2 + step * chunks + c, wbuf.at[step, c], rows)
        gather.start()
        return gather

    def first(c):
        def body(b, here):
            resid = rvec[c, here, :]
            z = precond(b, resid)
            pvec[c, here, :] = z
            xvec[c, here, :] = jnp.zeros((block, LANES), F32)
            pcat[c, here, :] = split_cat(z)
            return rows8(resid * z)

        return total(over_blocks(body))

    def update(step, c, rz):
        pw = total(over_blocks(lambda b, here: rows8(pvec[c, here, :] * wbuf[step, c, here, :])))
        alpha = rz / pw

        def body(b, here):
            resid = rvec[c, here, :] - alpha * wbuf[step, c, here, :]
            rvec[c, here, :] = resid
            xvec[c, here, :] = xvec[c, here, :] + alpha * pvec[c, here, :]
            z = precond(b, resid)
            zvec[here, :] = z
            return rows8(resid * z)

        rz_next = total(over_blocks(body))
        beta = rz_next / rz

        @pl.loop(0, nblk)
        def _(b):
            here = pl.ds(pl.multiple_of(b * block, block), block)
            p = zvec[here, :] + beta * pvec[c, here, :]
            pvec[c, here, :] = p
            pcat[c, here, :] = split_cat(p)

        return rz_next

    rz, flight, earlier = [], [], None
    for c in range(chunks):
        rz.append(first(c))
        earlier = send_image(0, c, earlier)
        flight.append(earlier)

    for step in range(ITERS - 2):
        for c in range(chunks):
            flight[c].finish()
            rz[c] = update(step, c, rz[c])
            earlier = send_image(step + 1, c, earlier)
            flight[c] = earlier

    def conclude(c, sums, base, slope):
        for copy in sums:
            copy.wait_recv()
        alpha = rz[c] / total(rows8(pw_buf[c]))
        corr_pieces[c * LANES : (c + 1) * LANES, :] = (base + alpha * slope).T
        resid_out[0, :, c * LANES : (c + 1) * LANES] = (
            rvec[c, pl.ds(pl.multiple_of(me * rows, 8), rows), :] - alpha * wlast[c]
        )

    for c in range(chunks):
        if c == chunks - 1 and chunks == 1:
            earlier.forward()
        flight[c].finish()
        rz[c] = update(ITERS - 2, c, rz[c])
        if c == chunks - 2:
            earlier.forward()

        def store(start, value, c=c):
            wlast[c, pl.ds(pl.multiple_of(start, 8), tile), :] = value

        matvec(c, store)

        def partial(t, acc, c=c):
            here = pl.ds(pl.multiple_of(t * block, block), block)
            there = pl.ds(pl.multiple_of(me * rows + t * block, 8), block)
            return acc + rows8(pvec[c, there, :] * wlast[c, here, :])

        pw_buf[c, pl.ds(pl.multiple_of(me * 8, 8), 8), :] = lax.fori_loop(
            0, per, partial, jnp.zeros((8, LANES), F32)
        )
        sums = small_gather(2 + c, pw_buf.at[c], 8)

        @pl.loop(0, nblk)
        def _(b, c=c):
            here = pl.ds(pl.multiple_of(b * block, block), block)
            xcat[here, :] = split_cat(xvec[c, here, :])

        base = fold(dot(pick[...], xcat[...]))
        slope = fold(dot(pick[...], pcat[c]))
        conclude(c, sums, base, slope)
    back = exchange(1, corr_pieces, corr_back)
    for copy in back:
        copy.wait_recv()
    for part in range(no):
        corr_out[:, part * piece : (part + 1) * piece] = corr_back[
            part * quota : (part + 1) * quota, :
        ]
    for copy in pending:
        copy.wait_send()


def shards(no, ns, residual, counts, assembly, level_two, block_inverse):
    _, slots, prim, width = assembly.shape
    rows = level_two.shape[1]
    block = block_inverse.shape[2]
    local = slots * prim
    quota = residual.shape[0]
    rhs = quota * no
    chunks = rhs // LANES
    nblk = width // block
    per = rows // block
    kinds = 6 if ns == 4 else ns - 1
    vmem = pl.BlockSpec(memory_space=pltpu.VMEM)
    dma = pltpu.SemaphoreType.DMA
    dims = (no, ns, rows, width, block, local, rhs)
    return pl.pallas_call(
        functools.partial(kernel, dims),
        out_shape=(
            jax.ShapeDtypeStruct(residual.shape, F32),
            jax.ShapeDtypeStruct((1, rows, rhs), F32),
        ),
        in_specs=[vmem, pl.BlockSpec(memory_space=pltpu.SMEM)]
        + [pl.BlockSpec(memory_space=pl.ANY)] * 3,
        out_specs=(vmem, vmem),
        scratch_shapes=[
            pltpu.VMEM((rows, width), F32),
            pltpu.VMEM((rows, width), BF16),
            pltpu.VMEM((rows, width), BF16),
            pltpu.VMEM((chunks, width, 2 * LANES), BF16),
            pltpu.VMEM((chunks, width, LANES), F32),
            pltpu.VMEM((chunks, width, LANES), F32),
            pltpu.VMEM((chunks, width, LANES), F32),
            pltpu.VMEM((width, LANES), F32),
            pltpu.VMEM((ITERS - 1, chunks, width, LANES), F32),
            pltpu.VMEM((chunks, rows, LANES), F32),
            pltpu.VMEM((ns * block, rows), F32),
            pltpu.VMEM((nblk, block, block), BF16),
            pltpu.VMEM((nblk, block, block), BF16),
            pltpu.VMEM((ns * 8, local), F32),
            pltpu.VMEM((rhs, local), F32),
            pltpu.VMEM((rhs, local), F32),
            pltpu.VMEM((ns * local, rhs), F32),
            pltpu.VMEM((ns * local, 2 * rhs), BF16),
            pltpu.VMEM((width, 2 * LANES), BF16),
            pltpu.VMEM((local, width), BF16),
            pltpu.VMEM((chunks, ns * 8, LANES), F32),
            pltpu.VMEM((rhs, local), F32),
            pltpu.VMEM((rhs, local), F32),
            pltpu.VMEM((prim, slots, width), jnp.int32),
            pltpu.VMEM((local, LANES), F32),
            dma,
            dma,
            dma,
            dma((2 + (ITERS - 1) * chunks, kinds)),
            dma((2 + (ITERS - 1) * chunks, kinds)),
            dma((2 + chunks, ns - 1)),
            dma((2 + chunks, ns - 1)),
            dma((2, no - 1)),
            dma((2, no - 1)),
        ],
        compiler_params=pltpu.CompilerParams(
            collective_id=0, has_side_effects=True, vmem_limit_bytes=60 * 1024 * 1024
        ),
    )(
        residual,
        counts,
        jnp.swapaxes(assembly, 1, 2),
        jnp.swapaxes(block_inverse, 1, 2),
        level_two,
    )


def solution(mesh):
    in_specs = (
        P("owner", "sub"),
        P("owner", "sub"),
        P("owner", "sub", None, None),
        P("owner", "sub", None),
        P("owner", "sub", None),
    )
    out_specs = (P("owner", "sub"), P("owner", "sub", None))
    body = functools.partial(shards, mesh.shape["owner"], mesh.shape["sub"])
    return jax.shard_map(body, mesh=mesh, in_specs=in_specs, out_specs=out_specs, check_vma=False)
```

profile of v0, /device:TPU:0, one launch (start us, length us, event | category | flops | bytes accessed | tf_op | source)
XLA Modules:
  0.0 110.3 jit_solution(2398683544660830755)
XLA Ops:
  0.6 106.2 %shard_map.68 = (f32[32,1152]{1,0:T(8,128)}, f32[1,576,256]{2,1,0:T(8,128)}) custom-call(f32[32,1152]{1,0:T(8,128)} %res_ref.1, s32[1,4]{1,0:T(1,128)} %counts_ref.1, s32[1,36,4,2304]{3,2,1,0:T(4,128)} %bitcast.2, f32[1,144,576]{2,1,0:T(8,128)} %bitcast.3, f32[1,576,2304]{2,1,0:T(8,128)} %mat_hbm.1), custom_call_target="tpu_custom_call" | custom-call | tf_op jit(solution)/shard_map/pallas_call | solution.py:437
  106.8 1.6 %copy.9 = f32[32,1152]{1,0:T(8,128)} copy(f32[32,1152]{1,0:T(8,128)} %get-tuple-element.4) | data formatting | bytes 294912
  108.4 1.9 %copy.10 = f32[1,576,256]{2,1,0:T(8,128)} copy(f32[1,576,256]{2,1,0:T(8,128)} %get-tuple-element.5) | data formatting | bytes 1179648
where the time goes:
time: 111 us; the launch traced here: 110 us
  Pallas kernels  106 us (95%)
  local copies, waits for them, and re-layouts  3.5 us (3%)
    pallas_call x1, Pallas kernels, shards(): pl.pallas_call(functools.partial(kernel, dims), out_shape=(jax.ShapeDtype...  106 us
    unnamed x2, local copies, waits for them, and re-layouts  3.5 us

commit v1 on v0

v1 whole, which is shorter than its diff:
```python
import functools

import jax
import jax.numpy as jnp
from jax import lax
from jax.experimental import pallas as pl
from jax.experimental.pallas import tpu as pltpu
from jax.sharding import PartitionSpec as P

ITERS = 4
LANES = 128
MESH = pl.DeviceIdType.MESH
F32 = jnp.float32
BF16 = jnp.bfloat16


def split(value):
    high = value.astype(BF16)
    return high, (value - high.astype(F32)).astype(BF16)


def split_cat(value):
    return jnp.concatenate(split(value), axis=1)


def fold(value):
    return value[:, :LANES] + value[:, LANES:]


def rows8(value):
    return jnp.sum(value.reshape(value.shape[0] // 8, 8, value.shape[1]), axis=0)


def dot(left, right):
    return jnp.dot(left, right, preferred_element_type=F32)


def total(acc):
    return jnp.sum(acc, axis=0, keepdims=True)


def iota(shape, axis):
    return lax.broadcasted_iota(jnp.int32, shape, axis)


def piece_dims(local, quota):
    wide = local - local % LANES
    rest = local % LANES
    return wide, rest, quota + (8 if rest else 0)


def kernel(
    dims,
    res_hbm,
    counts_ref,
    hot_hbm,
    inv_hbm,
    mat_hbm,
    corr_out,
    resid_out,
    res,
    mat,
    mat_hi,
    mat_lo,
    zcat,
    rvec,
    zloc,
    ploc,
    wbuf,
    wlast,
    inv_own,
    inv_pack,
    inv_hi,
    inv_lo,
    tbuf,
    trow,
    send_pieces,
    recv_pieces,
    lbuf,
    lcat,
    hotmat,
    pick,
    ypick,
    corr,
    pw_buf,
    corr_pieces,
    corr_back,
    hot_own,
    tcol,
    res_sem,
    mat_sem,
    inv_sem,
    hot_sem,
    sub_send,
    sub_recv,
    small_send,
    small_recv,
    own_send,
    own_recv,
):
    no, ns, rows, width, block, local, rhs = dims
    chunks = rhs // LANES
    nblk = width // block
    per = rows // block
    quota = rhs // no
    half = block // 2
    wide, rest, slab = piece_dims(local, quota)
    parts = LANES // quota
    mo = lax.axis_index("owner")
    me = lax.axis_index("sub")
    relay = ns == 4
    xn = me + 1 - 2 * lax.rem(me, 2)
    yn = lax.rem(me + 2, ns)
    far = 3 - me
    pending = []

    def at(ref, start, size):
        return ref.at[pl.ds(pl.multiple_of(start, 8), size)]

    def span(start, size):
        return pl.ds(pl.multiple_of(start, 8), size)

    def remote(src, dst, ssem, rsem, where):
        return pltpu.make_async_remote_copy(
            src_ref=src, dst_ref=dst, send_sem=ssem, recv_sem=rsem, device_id=where,
            device_id_type=MESH,
        )

    res_copy = pltpu.make_async_copy(res_hbm, res, res_sem)
    hot_copy = pltpu.make_async_copy(hot_hbm.at[0], hot_own, hot_sem)
    inv_copy = pltpu.make_async_copy(inv_hbm.at[0], inv_own, inv_sem)
    mat_copy = pltpu.make_async_copy(mat_hbm.at[0], mat, mat_sem)
    res_copy.start()
    hot_copy.start()
    inv_copy.start()
    mat_copy.start()

    barrier = pltpu.get_barrier_semaphore()
    for step in range(1, ns):
        pl.semaphore_signal(
            barrier, inc=1, device_id={"sub": lax.rem(me + step, ns)}, device_id_type=MESH
        )
    for step in range(1, no):
        pl.semaphore_signal(
            barrier, inc=1, device_id={"owner": lax.rem(mo + step, no)}, device_id_type=MESH
        )

    class Gather:
        def __init__(self, index, buf, size):
            self.index, self.buf, self.size = index, buf, size
            self.cut = (size // 2 + 7) // 8 * 8
            self.copies = []
            self.sent_on = False

        def part(self, who, part):
            if part == 0:
                return at(self.buf, who * self.size, self.cut)
            return at(self.buf, who * self.size + self.cut, self.size - self.cut)

        def add(self, kind, piece, peer):
            copy = remote(
                piece, piece, sub_send.at[self.index, kind], sub_recv.at[self.index, kind],
                {"sub": peer},
            )
            copy.start()
            self.copies.append(copy)
            pending.append(copy)

        def start(self):
            if relay:
                for kind, (peer, part) in enumerate(((xn, 0), (yn, 1), (xn, 1), (yn, 0))):
                    self.add(kind, self.part(me, part), peer)
            else:
                mine = at(self.buf, me * self.size, self.size)
                for step in range(1, ns):
                    self.add(step - 1, mine, lax.rem(me + step, ns))

        def forward(self):
            if relay and not self.sent_on:
                self.copies[0].wait_recv()
                self.add(4, self.part(xn, 0), yn)
                self.copies[1].wait_recv()
                self.add(5, self.part(yn, 1), xn)
            self.sent_on = True

        def pieces(self):
            size, cut = self.size, self.cut
            if relay:
                return [
                    (None, xn * size, cut),
                    (None, yn * size + cut, size - cut),
                    (self.copies[2], xn * size + cut, size - cut),
                    (self.copies[3], yn * size, cut),
                    (self.copies[4], far * size, cut),
                    (self.copies[5], far * size + cut, size - cut),
                ]
            return [
                (self.copies[step - 1], lax.rem(me + ns - step, ns) * size, size)
                for step in range(1, ns)
            ]

        def finish(self):
            self.forward()
            for copy, _, _ in self.pieces():
                if copy is not None:
                    copy.wait_recv()

    def small_gather(index, buf, size):
        copies = []
        for step in range(1, ns):
            mine = at(buf, me * size, size)
            copy = remote(
                mine, mine, small_send.at[index, step - 1], small_recv.at[index, step - 1],
                {"sub": lax.rem(me + step, ns)},
            )
            copy.start()
            copies.append(copy)
            pending.append(copy)
        return copies

    def owner_copy(index, src, dst, peer):
        return remote(
            at(src, peer * slab, slab), at(dst, mo * slab, slab),
            own_send.at[index, peer], own_recv.at[index, mo], {"owner": peer},
        )

    def owner_wait(index, dst, peer):
        @pl.when(mo != peer)
        def _():
            piece = at(dst, peer * slab, slab)
            remote(
                piece, piece, own_send.at[index, peer], own_recv.at[index, peer],
                {"owner": peer},
            ).wait_recv()

    hot_copy.wait()
    prim, slots = hot_own.shape[0], hot_own.shape[1]
    for q in range(slots):
        acc = jnp.zeros((prim, LANES), F32)
        spot = iota((prim, LANES), 1)
        for lane in range(0, width, LANES):
            acc += (hot_own[:, q, lane : lane + LANES] * (spot + lane)).astype(F32)
        value = jnp.sum(acc, axis=1, keepdims=True)
        alive = iota((prim, 1), 0) < counts_ref[0, q]
        tcol[q * prim : (q + 1) * prim, :] = jnp.broadcast_to(
            jnp.where(alive, value, -1.0), (prim, LANES)
        )
    tbuf[span(me * 8, 8), :] = tcol[...].T[:8, :]

    res_copy.wait()
    for part in range(no):
        low = part * local
        send_pieces[part * slab : part * slab + quota, :] = res[:, low : low + wide]
        if rest:
            strips = [
                res[t : t + 8, low + wide : low + local] for t in range(0, quota, 8)
            ]
            strips.append(jnp.zeros((8, wide - rest * len(strips)), F32))
            send_pieces[part * slab + quota : (part + 1) * slab, :] = jnp.concatenate(
                strips, axis=1
            )

    pl.semaphore_wait(barrier, ns - 1 + no - 1)

    for step in range(1, no):
        copy = owner_copy(0, send_pieces, recv_pieces, lax.rem(mo + step, no))
        copy.start()
        pending.append(copy)
    targets = small_gather(0, tbuf, 8)
    recv_pieces[span(mo * slab, slab), :] = send_pieces[span(mo * slab, slab), :]

    inv_copy.wait()
    prow, pcol = iota((half, block), 0), iota((half, block), 1)
    segments, diagonals = [], []
    for q in range(per):
        top = inv_own[:half, q * block : (q + 1) * block]
        last = jnp.concatenate(
            [
                inv_own[half:block, q * block + half : (q + 1) * block],
                jnp.zeros((half, block - half), F32),
            ],
            axis=1,
        )
        segments.append(jnp.where(pcol >= prow, top, last))
        diagonals.append(jnp.sum(jnp.where(pcol == prow, last, 0.0), axis=1, keepdims=True))
    pad = inv_pack.shape[1] - rows - per
    inv_pack[span(me * half, half), :] = jnp.concatenate(
        segments + diagonals + [jnp.zeros((half, pad), F32)], axis=1
    )
    inv_gather = Gather(0, inv_pack, half)
    inv_gather.start()

    mat_copy.wait()
    strip = 48

    @pl.loop(0, rows // strip)
    def _(t):
        here = span(t * strip, strip)
        high, low = split(mat[here, :])
        mat_hi[here, :] = high
        mat_lo[here, :] = low

    inv_gather.forward()

    local_gathers = []
    for c in range(chunks):
        owners = range(c * parts, (c + 1) * parts)
        for o in owners:
            owner_wait(0, recv_pieces, o)
        body = jnp.concatenate(
            [recv_pieces[o * slab : o * slab + quota, :] for o in owners], axis=0
        )
        lbuf[c, span(me * local, wide), :] = body.T
        if rest:
            ends = jnp.concatenate(
                [
                    recv_pieces[o * slab + quota : (o + 1) * slab, t * rest : (t + 1) * rest]
                    for o in owners
                    for t in range(quota // 8)
                ],
                axis=0,
            )
            lbuf[c, span(me * local + wide, rest), :] = ends.T
        gather = Gather(1 + c, lbuf.at[c], local)
        gather.start()
        local_gathers.append(gather)

    for lane in range(0, width, 2 * LANES):
        spot = iota((local, 2 * LANES), 1).astype(F32) + float(lane)
        pick[:, lane : lane + 2 * LANES] = jnp.where(spot == tcol[:, :1], 1.0, 0.0).astype(BF16)

    for copy in targets:
        copy.wait_recv()
    trow[...] = jnp.broadcast_to(
        jnp.concatenate([tbuf[s * 8 : s * 8 + 1, :] for s in range(ns)], axis=1), trow.shape
    )

    @pl.loop(0, width // strip)
    def _(t):
        spot = (iota((strip, ns * local), 0) + t * strip).astype(F32)
        hotmat[span(t * strip, strip), :] = jnp.where(spot == trow[:1, :], 1.0, 0.0).astype(BF16)

    local_gathers[0].forward()
    inv_gather.finish()

    @pl.loop(0, ns)
    def _(s):
        packed = inv_pack.at[span(s * half, half)]
        brow, bcol = iota((block, block), 0), iota((block, block), 1)
        for q in range(per):
            segment = packed[:, q * block : (q + 1) * block]
            ends = packed[:, rows + q : rows + q + 1]
            top = jnp.where(pcol >= prow, segment, 0.0)
            last = jnp.where(pcol < prow, segment, jnp.where(pcol == prow, ends, 0.0))
            low = jnp.concatenate(
                [jnp.zeros((half, half), F32), last[:, : block - half]], axis=1
            )
            one = jnp.concatenate([top, low], axis=0)
            high, low = split(jnp.where(brow == bcol, one, one + one.T))
            inv_hi[s * per + q] = high
            inv_lo[s * per + q] = low

    for gather in local_gathers[1:]:
        gather.forward()

    def precond(b, resid):
        rcat = split_cat(resid)
        return fold(dot(inv_hi[b], rcat) + dot(inv_lo[b], rcat))

    def first(c):
        lcat[...] = split_cat(lbuf[c])

        def one(b):
            here = span(b * block, block)
            resid = fold(dot(hotmat[here, :], lcat[...]))
            rvec[c, here, :] = resid
            z = precond(b, resid)
            zcat[c, here, :] = split_cat(z)
            return z, rows8(resid * z)

        acc = jnp.zeros((8, LANES), F32)
        for q in range(per):
            z, part = one(me * per + q)
            zloc[c, q * block : (q + 1) * block, :] = z
            acc = acc + part
        group = 4 if (nblk - per) % 4 == 0 else 3 if (nblk - per) % 3 == 0 else 1

        def step(t, acc):
            for u in range(group):
                acc = acc + one(lax.rem(me * per + per + t * group + u, nblk))[1]
            return acc

        return total(lax.fori_loop(0, (nblk - per) // group, step, acc))

    def update(k, c, gather, sums, rz):
        for copy in sums:
            copy.wait_recv()
        alpha = rz / total(rows8(pw_buf[k, c]))
        corr[c] = alpha * ypick[c] + (corr[c] if k else 0.0)

        def one(b):
            here = span(b * block, block)
            resid = rvec[c, here, :] - alpha * wbuf[k, c, here, :]
            rvec[c, here, :] = resid
            z = precond(b, resid)
            zcat[c, here, :] = split_cat(z)
            return z, rows8(resid * z)

        acc = jnp.zeros((8, LANES), F32)
        for q in range(per):
            z, part = one(me * per + q)
            zloc[c, q * block : (q + 1) * block, :] = z
            acc = acc + part
        gather.forward()
        for copy, start, size in gather.pieces():
            if copy is not None:
                copy.wait_recv()
            for u in range(size // block):
                acc = acc + one(start // block + u)[1]
        rz_next = total(acc)
        return rz_next, rz_next / rz

    tile = 2 * block if rows % (2 * block) == 0 else block

    def image(k, c, beta):
        def body(t, acc):
            here = span(t * tile, tile)
            there = span(me * rows + t * tile, tile)
            w = fold(dot(mat_hi[here, :], zcat[c]) + dot(mat_lo[here, :], zcat[c]))
            p = zloc[c, here, :]
            if k:
                w = w + beta * wbuf[k - 1, c, there, :]
                p = p + beta * ploc[c, here, :]
            ploc[c, here, :] = p
            if k < ITERS - 1:
                wbuf[k, c, there, :] = w
            else:
                wlast[c, here, :] = w
            return acc + rows8(p * w)

        acc = lax.fori_loop(0, rows // tile, body, jnp.zeros((8, LANES), F32))
        pw_buf[k, c, span(me * 8, 8), :] = acc
        return small_gather(1 + k * chunks + c, pw_buf.at[k, c], 8)

    def spread(k, c, earlier):
        if earlier is not None:
            earlier.forward()
        gather = Gather(1 + chunks + k * chunks + c, wbuf.at[k, c], rows)
        gather.start()
        return gather

    def picked(k, c, beta):
        y = fold(dot(pick[...], zcat[c]))
        ypick[c] = y + beta * ypick[c] if k else y

    def conclude(c, sums, rz):
        for copy in sums:
            copy.wait_recv()
        alpha = rz / total(rows8(pw_buf[ITERS - 1, c]))
        value = corr[c] + alpha * ypick[c]
        owners = range(c * parts, (c + 1) * parts)
        body = value[:wide, :].T
        ends = value[wide:, :].T if rest else None
        for o in owners:
            low = (o - c * parts) * quota
            corr_pieces[o * slab : o * slab + quota, :] = body[low : low + quota, :]
            if rest:
                strips = [ends[low + t : low + t + 8, :] for t in range(0, quota, 8)]
                strips.append(jnp.zeros((8, wide - rest * len(strips)), F32))
                corr_pieces[o * slab + quota : (o + 1) * slab, :] = jnp.concatenate(
                    strips, axis=1
                )
        for o in owners:
            @pl.when(mo != o)
            def _(o=o):
                owner_copy(1, corr_pieces, corr_back, o).start()
        resid_out[0, :, c * LANES : (c + 1) * LANES] = (
            rvec[c, span(me * rows, rows), :] - alpha * wlast[c]
        )

    rz, beta = [None] * chunks, [None] * chunks
    sums, flight, earlier = [None] * chunks, [None] * chunks, None
    for c in range(chunks):
        local_gathers[c].finish()
        rz[c] = first(c)
        sums[c] = image(0, c, None)
        earlier = flight[c] = spread(0, c, earlier)
        picked(0, c, None)

    for k in range(ITERS - 1):
        final = k == ITERS - 2
        for c in range(chunks):
            if final and c:
                earlier.forward()
                conclude(c - 1, sums[c - 1], rz[c - 1])
            rz[c], beta[c] = update(k, c, flight[c], sums[c], rz[c])
            sums[c] = image(k + 1, c, beta[c])
            if not final:
                earlier = flight[c] = spread(k + 1, c, earlier)
            picked(k + 1, c, beta[c])
    conclude(chunks - 1, sums[-1], rz[-1])

    corr_back[span(mo * slab, slab), :] = corr_pieces[span(mo * slab, slab), :]
    for part in range(no):
        owner_wait(1, corr_back, part)
        low = part * local
        corr_out[:, low : low + wide] = corr_back[part * slab : part * slab + quota, :]
        for t in range(quota // 8 if rest else 0):
            corr_out[8 * t : 8 * t + 8, low + wide : low + local] = corr_back[
                part * slab + quota : (part + 1) * slab, t * rest : (t + 1) * rest
            ]
    for copy in pending:
        copy.wait_send()
    for o in range(no):
        @pl.when(mo != o)
        def _(o=o):
            owner_copy(1, corr_pieces, corr_back, o).wait_send()


def shards(no, ns, residual, counts, assembly, level_two, block_inverse):
    _, slots, prim, width = assembly.shape
    rows = level_two.shape[1]
    block = block_inverse.shape[2]
    local = slots * prim
    quota = residual.shape[0]
    rhs = quota * no
    chunks = rhs // LANES
    nblk = width // block
    per = rows // block
    half = block // 2
    wide, _, slab = piece_dims(local, quota)
    packed = pl.cdiv(rows + per, LANES) * LANES
    kinds = 6 if ns == 4 else ns - 1
    vmem = pl.BlockSpec(memory_space=pltpu.VMEM)
    anywhere = pl.BlockSpec(memory_space=pl.ANY)
    dma = pltpu.SemaphoreType.DMA
    dims = (no, ns, rows, width, block, local, rhs)
    return pl.pallas_call(
        functools.partial(kernel, dims),
        out_shape=(pltpu.VMEM(residual.shape, F32), pltpu.VMEM((1, rows, rhs), F32)),
        in_specs=[anywhere, pl.BlockSpec(memory_space=pltpu.SMEM)] + [anywhere] * 3,
        out_specs=(vmem, vmem),
        scratch_shapes=[
            pltpu.VMEM(residual.shape, F32),
            pltpu.VMEM((rows, width), F32),
            pltpu.VMEM((rows, width), BF16),
            pltpu.VMEM((rows, width), BF16),
            pltpu.VMEM((chunks, width, 2 * LANES), BF16),
            pltpu.VMEM((chunks, width, LANES), F32),
            pltpu.VMEM((chunks, rows, LANES), F32),
            pltpu.VMEM((chunks, rows, LANES), F32),
            pltpu.VMEM((ITERS - 1, chunks, width, LANES), F32),
            pltpu.VMEM((chunks, rows, LANES), F32),
            pltpu.VMEM((block, rows), F32),
            pltpu.VMEM((ns * half, packed), F32),
            pltpu.VMEM((nblk, block, block), BF16),
            pltpu.VMEM((nblk, block, block), BF16),
            pltpu.VMEM((ns * 8, local), F32),
            pltpu.VMEM((8, ns * local), F32),
            pltpu.VMEM((no * slab, wide), F32),
            pltpu.VMEM((no * slab, wide), F32),
            pltpu.VMEM((chunks, ns * local, LANES), F32),
            pltpu.VMEM((ns * local, 2 * LANES), BF16),
            pltpu.VMEM((width, ns * local), BF16),
            pltpu.VMEM((local, width), BF16),
            pltpu.VMEM((chunks, local, LANES), F32),
            pltpu.VMEM((chunks, local, LANES), F32),
            pltpu.VMEM((ITERS, chunks, ns * 8, LANES), F32),
            pltpu.VMEM((no * slab, wide), F32),
            pltpu.VMEM((no * slab, wide), F32),
            pltpu.VMEM((prim, slots, width), jnp.int32),
            pltpu.VMEM((local, LANES), F32),
            dma,
            dma,
            dma,
            dma,
            dma((1 + ITERS * chunks, kinds)),
            dma((1 + ITERS * chunks, kinds)),
            dma((1 + ITERS * chunks, ns - 1)),
            dma((1 + ITERS * chunks, ns - 1)),
            dma((2, no)),
            dma((2, no)),
        ],
        compiler_params=pltpu.CompilerParams(
            collective_id=0, has_side_effects=True, vmem_limit_bytes=60 * 1024 * 1024
        ),
    )(
        residual,
        counts,
        jnp.swapaxes(assembly, 1, 2),
        jnp.swapaxes(block_inverse, 1, 2),
        level_two,
    )


def solution(mesh):
    in_specs = (
        P("owner", "sub"),
        P("owner", "sub"),
        P("owner", "sub", None, None),
        P("owner", "sub", None),
        P("owner", "sub", None),
    )
    out_specs = (P("owner", "sub"), P("owner", "sub", None))
    body = functools.partial(shards, mesh.shape["owner"], mesh.shape["sub"])
    return jax.shard_map(body, mesh=mesh, in_specs=in_specs, out_specs=out_specs, check_vma=False)
```

time: 111 us -> 97.5 us (0.88)
  Pallas kernels: 106 us -> 95.2 us
  local copies, waits for them, and re-layouts: 3.5 us -> 1.48 us
    pallas_call x1, Pallas kernels: 106 us -> 95.2 us  [shards(): pl.pallas_call(functools.partial(kernel, dims), out_shape=(pltpu.VMEM(res...]
    unnamed x2, local copies, waits for them, and re-layouts: 3.5 us -> 1.48 us
where the time goes in v1:
time: 97.5 us; the launch traced here: 97.3 us
  Pallas kernels  95.2 us (98%)
  local copies, waits for them, and re-layouts  1.48 us (2%)
    pallas_call x1, Pallas kernels, shards(): pl.pallas_call(functools.partial(kernel, dims), out_shape=(pltpu.VMEM(res...  95.2 us

profile of v1, /device:TPU:0, one launch (start us, length us, event | category | flops | bytes accessed | tf_op | source)
XLA Modules:
  0.0 97.3 jit_solution(11228950290659439805)
XLA Ops:
  0.6 95.2 %shard_map.68 = (f32[32,1152]{1,0:T(8,128)S(1)}, f32[1,576,256]{2,1,0:T(8,128)S(1)}) custom-call(f32[32,1152]{1,0:T(8,128)} %res_hbm.1, s32[1,4]{1,0:T(1,128)} %counts_ref.1, s32[1,36,4,2304]{3,2,1,0:T(4,128)} %bitcast.2, f32[1,144,576]{2,1,0:T(8,128)} %bitcast.3, f32[1,576,2304]{2,1,0:T(8,128)} %mat_hbm.1), custom_call_target="tpu_custom_call" | custom-call | tf_op jit(solution)/shard_map/pallas_call | solution.py:538
  95.9 0.7 copy.9
  96.5 0.8 copy.10

commit v2 on v1

--- a/solution.py
+++ b/solution.py
@@ -41,6 +41,13 @@
 
 def iota(shape, axis):
     return lax.broadcasted_iota(jnp.int32, shape, axis)
+
+
+def chunk_owners(chunks, parts, c):
+    if chunks != 2 or parts % 2:
+        return list(range(c * parts, (c + 1) * parts))
+    side = parts // 2
+    return [t * side + u for t in ((0, 2), (3, 1))[c] for u in range(side)]
 
 
 def piece_dims(local, quota):
@@ -73,7 +80,6 @@
     inv_hi,
     inv_lo,
     tbuf,
-    trow,
     send_pieces,
     recv_pieces,
     lbuf,
@@ -149,7 +155,7 @@
         def __init__(self, index, buf, size):
             self.index, self.buf, self.size = index, buf, size
             self.cut = (size // 2 + 7) // 8 * 8
-            self.copies = []
+            self.copies = {}
             self.sent_on = False
 
         def part(self, who, part):
@@ -163,8 +169,12 @@
                 {"sub": peer},
             )
             copy.start()
-            self.copies.append(copy)
+            self.copies[kind] = copy
             pending.append(copy)
+
+        def start_part(self, part):
+            for kind in ((0, 3), (1, 2))[part]:
+                self.add(kind, self.part(me, part), xn if kind in (0, 2) else yn)
 
         def start(self):
             if relay:
@@ -199,11 +209,14 @@
                 for step in range(1, ns)
             ]
 
-        def finish(self):
-            self.forward()
-            for copy, _, _ in self.pieces():
-                if copy is not None:
-                    copy.wait_recv()
+        def runs(self):
+            kinds = ((2,), (3,), (4, 5)) if relay else [(step - 1,) for step in range(1, ns)]
+            peers = (xn, yn, far) if relay else [lax.rem(me + ns - step, ns) for step in range(1, ns)]
+            return list(zip(peers, kinds))
+
+        def finish(self, kinds):
+            for kind in kinds:
+                self.copies[kind].wait_recv()
 
     def small_gather(index, buf, size):
         copies = []
@@ -233,20 +246,6 @@
                 {"owner": peer},
             ).wait_recv()
 
-    hot_copy.wait()
-    prim, slots = hot_own.shape[0], hot_own.shape[1]
-    for q in range(slots):
-        acc = jnp.zeros((prim, LANES), F32)
-        spot = iota((prim, LANES), 1)
-        for lane in range(0, width, LANES):
-            acc += (hot_own[:, q, lane : lane + LANES] * (spot + lane)).astype(F32)
-        value = jnp.sum(acc, axis=1, keepdims=True)
-        alive = iota((prim, 1), 0) < counts_ref[0, q]
-        tcol[q * prim : (q + 1) * prim, :] = jnp.broadcast_to(
-            jnp.where(alive, value, -1.0), (prim, LANES)
-        )
-    tbuf[span(me * 8, 8), :] = tcol[...].T[:8, :]
-
     res_copy.wait()
     for part in range(no):
         low = part * local
@@ -260,14 +259,19 @@
                 strips, axis=1
             )
 
-    pl.semaphore_wait(barrier, ns - 1 + no - 1)
-
-    for step in range(1, no):
-        copy = owner_copy(0, send_pieces, recv_pieces, lax.rem(mo + step, no))
-        copy.start()
-        pending.append(copy)
-    targets = small_gather(0, tbuf, 8)
-    recv_pieces[span(mo * slab, slab), :] = send_pieces[span(mo * slab, slab), :]
+    hot_copy.wait()
+    prim, slots = hot_own.shape[0], hot_own.shape[1]
+    for q in range(slots):
+        acc = jnp.zeros((prim, LANES), F32)
+        spot = iota((prim, LANES), 1)
+        for lane in range(0, width, LANES):
+            acc += (hot_own[:, q, lane : lane + LANES] * (spot + lane)).astype(F32)
+        value = jnp.sum(acc, axis=1, keepdims=True)
+        alive = iota((prim, 1), 0) < counts_ref[0, q]
+        tcol[q * prim : (q + 1) * prim, :] = jnp.broadcast_to(
+            jnp.where(alive, value, -1.0), (prim, LANES)
+        )
+    tbuf[span(me * 8, 8), :] = tcol[...].T[:8, :]
 
     inv_copy.wait()
     prow, pcol = iota((half, block), 0), iota((half, block), 1)
@@ -287,6 +291,23 @@
     inv_pack[span(me * half, half), :] = jnp.concatenate(
         segments + diagonals + [jnp.zeros((half, pad), F32)], axis=1
     )
+    pl.semaphore_wait(barrier, ns - 1 + no - 1)
+
+    targets = small_gather(0, tbuf, 8)
+    routed = [
+        owner_copy(0, send_pieces, recv_pieces, lax.rem(mo + step, no)) for step in range(1, no)
+    ]
+    pending.extend(routed)
+    mixed = chunks == 2 and parts % 2 == 0
+    early_owner = lax.rem(mo // (parts // 2), 2) == 0 if mixed else mo >= 0
+
+    @pl.when(early_owner)
+    def _():
+        for copy in routed:
+            copy.start()
+
+    recv_pieces[span(mo * slab, slab), :] = send_pieces[span(mo * slab, slab), :]
+
     inv_gather = Gather(0, inv_pack, half)
     inv_gather.start()
 
@@ -300,11 +321,13 @@
         mat_hi[here, :] = high
         mat_lo[here, :] = low
 
-    inv_gather.forward()
-
-    local_gathers = []
-    for c in range(chunks):
-        owners = range(c * parts, (c + 1) * parts)
+    @pl.when(jnp.logical_not(early_owner))
+    def _():
+        for copy in routed:
+            copy.start()
+
+    def arrange(c):
+        owners = chunk_owners(chunks, parts, c)
         for o in owners:
             owner_wait(0, recv_pieces, o)
         body = jnp.concatenate(
@@ -321,30 +344,9 @@
                 axis=0,
             )
             lbuf[c, span(me * local + wide, rest), :] = ends.T
-        gather = Gather(1 + c, lbuf.at[c], local)
-        gather.start()
-        local_gathers.append(gather)
-
-    for lane in range(0, width, 2 * LANES):
-        spot = iota((local, 2 * LANES), 1).astype(F32) + float(lane)
-        pick[:, lane : lane + 2 * LANES] = jnp.where(spot == tcol[:, :1], 1.0, 0.0).astype(BF16)
-
-    for copy in targets:
-        copy.wait_recv()
-    trow[...] = jnp.broadcast_to(
-        jnp.concatenate([tbuf[s * 8 : s * 8 + 1, :] for s in range(ns)], axis=1), trow.shape
-    )
-
-    @pl.loop(0, width // strip)
-    def _(t):
-        spot = (iota((strip, ns * local), 0) + t * strip).astype(F32)
-        hotmat[span(t * strip, strip), :] = jnp.where(spot == trow[:1, :], 1.0, 0.0).astype(BF16)
-
-    local_gathers[0].forward()
-    inv_gather.finish()
-
-    @pl.loop(0, ns)
-    def _(s):
+        return Gather(1 + c, lbuf.at[c], local)
+
+    def unpack(s):
         packed = inv_pack.at[span(s * half, half)]
         brow, bcol = iota((block, block), 0), iota((block, block), 1)
         for q in range(per):
@@ -360,37 +362,88 @@
             inv_hi[s * per + q] = high
             inv_lo[s * per + q] = low
 
-    for gather in local_gathers[1:]:
-        gather.forward()
+    def seed(c, s, fresh):
+        lcat[...] = split_cat(lbuf[c, span(s * local, local), :])
+
+        @pl.loop(0, ns)
+        def _(t):
+            here = span(t * rows, rows)
+            value = fold(dot(hotmat[s, here, :], lcat[...]))
+            rvec[c, here, :] = value if fresh else rvec[c, here, :] + value
+
+    unpack(me)
+    for lane in range(0, width, 2 * LANES):
+        spot = iota((local, 2 * LANES), 1).astype(F32) + float(lane)
+        pick[:, lane : lane + 2 * LANES] = jnp.where(spot == tcol[:, :1], 1.0, 0.0).astype(BF16)
+
+    local_gathers = [arrange(0)]
+    local_gathers[0].start()
+    inv_gather.forward()
+    for copy in targets:
+        copy.wait_recv()
+
+    @pl.loop(0, ns)
+    def _(s):
+        goal = tbuf[span(s * 8, 8), :][:1, :]
+        for row in range(0, width, block):
+            spot = (iota((block, local), 0) + row).astype(F32)
+            hotmat[s, row : row + block, :] = jnp.where(spot == goal, 1.0, 0.0).astype(BF16)
+
+    seed(0, me, True)
+    inv_runs = inv_gather.runs()
+    if relay:
+        s, kinds = inv_runs[0]
+        inv_gather.finish(kinds)
+        unpack(s)
+    local_gathers[0].forward()
+    if relay:
+        s, kinds = inv_runs[1]
+        inv_gather.finish(kinds)
+        unpack(s)
+    for c in range(1, chunks):
+        local_gathers.append(arrange(c))
+        local_gathers[c].start()
+    for s, kinds in local_gathers[0].runs()[:-1]:
+        local_gathers[0].finish(kinds)
+        seed(0, s, False)
+    if relay:
+        s, kinds = inv_runs[2]
+        inv_gather.finish(kinds)
+        unpack(s)
+    else:
+        for s, kinds in inv_runs:
+            inv_gather.finish(kinds)
+
+        @pl.loop(1, ns)
+        def _(t):
+            unpack(lax.rem(me + t, ns))
 
     def precond(b, resid):
         rcat = split_cat(resid)
         return fold(dot(inv_hi[b], rcat) + dot(inv_lo[b], rcat))
 
     def first(c):
-        lcat[...] = split_cat(lbuf[c])
-
-        def one(b):
-            here = span(b * block, block)
-            resid = fold(dot(hotmat[here, :], lcat[...]))
-            rvec[c, here, :] = resid
-            z = precond(b, resid)
-            zcat[c, here, :] = split_cat(z)
-            return z, rows8(resid * z)
-
-        acc = jnp.zeros((8, LANES), F32)
-        for q in range(per):
-            z, part = one(me * per + q)
-            zloc[c, q * block : (q + 1) * block, :] = z
-            acc = acc + part
-        group = 4 if (nblk - per) % 4 == 0 else 3 if (nblk - per) % 3 == 0 else 1
-
-        def step(t, acc):
-            for u in range(group):
-                acc = acc + one(lax.rem(me * per + per + t * group + u, nblk))[1]
+        last, kinds = local_gathers[c].runs()[-1]
+        local_gathers[c].finish(kinds)
+        lcat[...] = split_cat(lbuf[c, span(last * local, local), :])
+
+        def run(s, acc, own):
+            value = fold(dot(hotmat[last, span(s * rows, rows), :], lcat[...]))
+            value = rvec[c, span(s * rows, rows), :] + value
+            rvec[c, span(s * rows, rows), :] = value
+            for q in range(per):
+                resid = value[q * block : (q + 1) * block, :]
+                z = precond(s * per + q, resid)
+                zcat[c, span(s * rows + q * block, block), :] = split_cat(z)
+                if own:
+                    zloc[c, q * block : (q + 1) * block, :] = z
+                acc = acc + rows8(resid * z)
             return acc
 
-        return total(lax.fori_loop(0, (nblk - per) // group, step, acc))
+        acc = run(me, jnp.zeros((8, LANES), F32), True)
+        return total(
+            lax.fori_loop(1, ns, lambda t, acc: run(lax.rem(me + t, ns), acc, False), acc)
+        )
 
     def update(k, c, gather, sums, rz):
         for copy in sums:
@@ -422,7 +475,7 @@
 
     tile = 2 * block if rows % (2 * block) == 0 else block
 
-    def image(k, c, beta):
+    def image(k, c, beta, gather=None):
         def body(t, acc):
             here = span(t * tile, tile)
             there = span(me * rows + t * tile, tile)
@@ -438,14 +491,22 @@
                 wlast[c, here, :] = w
             return acc + rows8(p * w)
 
-        acc = lax.fori_loop(0, rows // tile, body, jnp.zeros((8, LANES), F32))
+        acc = jnp.zeros((8, LANES), F32)
+        if gather is None:
+            acc = lax.fori_loop(0, rows // tile, body, acc)
+        else:
+            for part in range(2):
+                acc = body(part, acc)
+                gather.start_part(part)
         pw_buf[k, c, span(me * 8, 8), :] = acc
         return small_gather(1 + k * chunks + c, pw_buf.at[k, c], 8)
 
+    def rows_gather(k, c):
+        return Gather(1 + chunks + k * chunks + c, wbuf.at[k, c], rows)
+
     def spread(k, c, earlier):
-        if earlier is not None:
-            earlier.forward()
-        gather = Gather(1 + chunks + k * chunks + c, wbuf.at[k, c], rows)
+        earlier.forward()
+        gather = rows_gather(k, c)
         gather.start()
         return gather
 
@@ -458,11 +519,11 @@
             copy.wait_recv()
         alpha = rz / total(rows8(pw_buf[ITERS - 1, c]))
         value = corr[c] + alpha * ypick[c]
-        owners = range(c * parts, (c + 1) * parts)
+        owners = chunk_owners(chunks, parts, c)
         body = value[:wide, :].T
         ends = value[wide:, :].T if rest else None
-        for o in owners:
-            low = (o - c * parts) * quota
+        for t, o in enumerate(owners):
+            low = t * quota
             corr_pieces[o * slab : o * slab + quota, :] = body[low : low + quota, :]
             if rest:
                 strips = [ends[low + t : low + t + 8, :] for t in range(0, quota, 8)]
@@ -474,17 +535,38 @@
             @pl.when(mo != o)
             def _(o=o):
                 owner_copy(1, corr_pieces, corr_back, o).start()
-        resid_out[0, :, c * LANES : (c + 1) * LANES] = (
-            rvec[c, span(me * rows, rows), :] - alpha * wlast[c]
-        )
+        left = rvec[c, span(me * rows, rows), :] - alpha * wlast[c]
+        if not mixed:
+            resid_out[0, :, c * LANES : (c + 1) * LANES] = left
+        elif c == 0:
+            wlast[c] = left
+        else:
+            side = iota(left.shape, 1) < LANES // 2
+            resid_out[0, :, :LANES] = jnp.where(side, wlast[0], left)
+            resid_out[0, :, LANES:] = pltpu.roll(jnp.where(side, left, wlast[0]), LANES // 2, 1)
 
     rz, beta = [None] * chunks, [None] * chunks
     sums, flight, earlier = [None] * chunks, [None] * chunks, None
     for c in range(chunks):
-        local_gathers[c].finish()
+        if c:
+            seed(c, me, True)
+            for s, kinds in local_gathers[c].runs()[:-1]:
+                local_gathers[c].finish(kinds)
+                seed(c, s, False)
         rz[c] = first(c)
-        sums[c] = image(0, c, None)
-        earlier = flight[c] = spread(0, c, earlier)
+        if c == 0:
+            for gather in local_gathers[1:]:
+                gather.forward()
+        if c:
+            earlier.forward()
+            sums[c] = image(0, c, None)
+            earlier = flight[c] = spread(0, c, earlier)
+        else:
+            earlier = flight[c] = rows_gather(0, c)
+            early = relay and tile * 2 == rows and tile == earlier.cut
+            sums[c] = image(0, c, None, earlier if early else None)
+            if not early:
+                earlier.start()
         picked(0, c, None)
 
     for k in range(ITERS - 1):
@@ -492,13 +574,13 @@
         for c in range(chunks):
             if final and c:
                 earlier.forward()
-                conclude(c - 1, sums[c - 1], rz[c - 1])
             rz[c], beta[c] = update(k, c, flight[c], sums[c], rz[c])
             sums[c] = image(k + 1, c, beta[c])
             if not final:
                 earlier = flight[c] = spread(k + 1, c, earlier)
             picked(k + 1, c, beta[c])
-    conclude(chunks - 1, sums[-1], rz[-1])
+    for c in range(chunks):
+        conclude(c, sums[c], rz[c])
 
     corr_back[span(mo * slab, slab), :] = corr_pieces[span(mo * slab, slab), :]
     for part in range(no):
@@ -556,12 +638,11 @@
             pltpu.VMEM((nblk, block, block), BF16),
             pltpu.VMEM((nblk, block, block), BF16),
             pltpu.VMEM((ns * 8, local), F32),
-            pltpu.VMEM((8, ns * local), F32),
             pltpu.VMEM((no * slab, wide), F32),
             pltpu.VMEM((no * slab, wide), F32),
             pltpu.VMEM((chunks, ns * local, LANES), F32),
-            pltpu.VMEM((ns * local, 2 * LANES), BF16),
-            pltpu.VMEM((width, ns * local), BF16),
+            pltpu.VMEM((local, 2 * LANES), BF16),
+            pltpu.VMEM((ns, width, local), BF16),
             pltpu.VMEM((local, width), BF16),
             pltpu.VMEM((chunks, local, LANES), F32),
             pltpu.VMEM((chunks, local, LANES), F32),

time: 97.5 us -> 93.8 us (0.962)
  Pallas kernels: 95.2 us -> 91.5 us
    pallas_call x1, Pallas kernels: 95.2 us -> 91.5 us  [shards(): pl.pallas_call(functools.partial(kernel, dims), out_shape=(pltpu.VMEM(res...]
where the time goes in v2:
time: 93.8 us; the launch traced here: 93.7 us
  Pallas kernels  91.5 us (98%)
  local copies, waits for them, and re-layouts  1.48 us (2%)
    pallas_call x1, Pallas kernels, shards(): pl.pallas_call(functools.partial(kernel, dims), out_shape=(pltpu.VMEM(res...  91.5 us

profile of v2, /device:TPU:0, one launch (start us, length us, event | category | flops | bytes accessed | tf_op | source)
XLA Modules:
  0.0 93.7 jit_solution(8967572195597104778)
XLA Ops:
  0.6 91.5 %shard_map.68 = (f32[32,1152]{1,0:T(8,128)S(1)}, f32[1,576,256]{2,1,0:T(8,128)S(1)}) custom-call(f32[32,1152]{1,0:T(8,128)} %res_hbm.1, s32[1,4]{1,0:T(1,128)} %counts_ref.1, s32[1,36,4,2304]{3,2,1,0:T(4,128)} %bitcast.2, f32[1,144,576]{2,1,0:T(8,128)} %bitcast.3, f32[1,576,2304]{2,1,0:T(8,128)} %mat_hbm.1), custom_call_target="tpu_custom_call" | custom-call | tf_op jit(solution)/shard_map/pallas_call | solution.py:620
  92.2 0.7 copy.9
  92.8 0.8 copy.10

commit v3 on v2

--- a/solution.py
+++ b/solution.py
@@ -567,6 +567,7 @@
             sums[c] = image(0, c, None, earlier if early else None)
             if not early:
                 earlier.start()
+    for c in range(chunks):
         picked(0, c, None)
 
     for k in range(ITERS - 1):

time: 93.8 us -> 94 us (level)
  no operation moved by 1% of the time
where the time goes in v3:
time: 94 us; the launch traced here: 93.7 us
  Pallas kernels  91.6 us (97%)
  local copies, waits for them, and re-layouts  1.48 us (2%)
    pallas_call x1, Pallas kernels, shards(): pl.pallas_call(functools.partial(kernel, dims), out_shape=(pltpu.VMEM(res...  91.6 us

profile of v3, /device:TPU:0, one launch (start us, length us, event | category | flops | bytes accessed | tf_op | source)
XLA Modules:
  0.0 93.7 jit_solution(2003061850556040023)
XLA Ops:
  0.6 91.6 %shard_map.68 = (f32[32,1152]{1,0:T(8,128)S(1)}, f32[1,576,256]{2,1,0:T(8,128)S(1)}) custom-call(f32[32,1152]{1,0:T(8,128)} %res_hbm.1, s32[1,4]{1,0:T(1,128)} %counts_ref.1, s32[1,36,4,2304]{3,2,1,0:T(4,128)} %bitcast.2, f32[1,144,576]{2,1,0:T(8,128)} %bitcast.3, f32[1,576,2304]{2,1,0:T(8,128)} %mat_hbm.1), custom_call_target="tpu_custom_call" | custom-call | tf_op jit(solution)/shard_map/pallas_call | solution.py:621
  92.2 0.7 copy.9
  92.9 0.8 copy.10
